TPU v7x, 256 devices: a whole 4x4x8 slice. The times are simulated.
256 devices in a mesh: ctx: 32 (over z, y), head: 8 (over x, core).
Axes of the slice: x: 4, y: 4, z: 8, core: 2. Of those that a mesh axis runs over, the one named last changes fastest.
Arguments:
- queries: bfloat16 [64, 32768, 128], P('head', 'ctx'), may hold values from -54.5 to 54.5
- key_heads: bfloat16 [8, 32768, 128], P('head', 'ctx'), may hold values from -6.8125 to 6.8125
- value_tensor: bfloat16 [8, 32768, 128], P('head', 'ctx'), may hold values from -6 to 6
- distance_use: int32 [32, 5], P('ctx'), may hold values 0 or 1
- block_pick: int32 [256, 5], P('ctx'), may hold values from 0 to 7
Outputs:
- attended: bfloat16 [64, 32768, 128], P(None, ('ctx', 'head'))
All inputs are finite; a program needn't handle non-finite values. No bound on the sum of `distance_use` on one device may be relied on, other than what follows from the above.
Results may differ from a plain program's by a relative error of at most 0.0029.
Values may be sent and summed in bfloat16 or wider, within the bound.
A program may use at most 64 MiB of HBM per device.

v0:
```python
import math

import jax
import jax.numpy as jnp
from jax import lax
from jax.sharding import PartitionSpec as P

BLOCK_TOKENS = 128


def from_behind(value, axis, steps):
    count = lax.axis_size(axis)
    initial, last = (max(0, -steps), min(count, count - steps))
    return lax.ppermute(value, axis, [(source, source + steps) for source in range(initial, last)])


def for_sending(value):
    return jax.tree.map(lambda a: a.astype(jnp.bfloat16) if a.dtype == jnp.float32 else a, value)


def attend(query_matrix, key_local, value_local, remote_key, remote_value, far_live):
    count_rows, head_width = query_matrix.shape
    row_block = min(512, count_rows)
    blocks_per = row_block // BLOCK_TOKENS
    score_scale = 1.0 / math.sqrt(head_width)
    pieces_out = []
    for group_index in range(count_rows // row_block):
        first_row = group_index * row_block
        last_row = first_row + row_block
        rows_now = query_matrix[first_row:last_row]
        near_scores = (
            jnp.einsum(
                "qd,kd->qk", rows_now, key_local[:last_row], preferred_element_type=jnp.float32
            )
            * score_scale
        )
        row_pos = first_row + lax.broadcasted_iota(jnp.int32, (row_block, last_row), 0)
        col_pos = lax.broadcasted_iota(jnp.int32, (row_block, last_row), 1)
        near_scores = jnp.where(col_pos <= row_pos, near_scores, -jnp.inf)
        first_block = first_row // BLOCK_TOKENS
        current_remote_keys = remote_key[first_block : first_block + blocks_per]
        far_values_now = remote_value[first_block : first_block + blocks_per]
        rows_of_block = rows_now.reshape(blocks_per, BLOCK_TOKENS, head_width)
        remote_scores = (
            jnp.einsum(
                "ghj,gcj->ghc",
                rows_of_block,
                current_remote_keys,
                preferred_element_type=jnp.float32,
            )
            * score_scale
        )
        remote_scores = jnp.where(far_live[None, None, :], remote_scores, -jnp.inf)
        row_peak = jnp.maximum(
            jnp.max(near_scores, axis=1, keepdims=True),
            jnp.max(remote_scores, axis=2).reshape(row_block, 1),
        )
        near_weights = jnp.exp(near_scores - row_peak)
        far_weights = jnp.exp(remote_scores - row_peak.reshape(blocks_per, BLOCK_TOKENS, 1))
        row_total = jnp.sum(near_weights, axis=1, keepdims=True) + jnp.sum(
            far_weights, axis=2
        ).reshape(row_block, 1)
        running_sum = jnp.dot(
            near_weights.astype(jnp.bfloat16),
            value_local[:last_row],
            preferred_element_type=jnp.float32,
        )
        far_summed = jnp.einsum(
            "mnf,mfq->mnq",
            far_weights.astype(jnp.bfloat16),
            far_values_now,
            preferred_element_type=jnp.float32,
        )
        running_sum = running_sum + far_summed.reshape(row_block, head_width)
        pieces_out.append((running_sum / row_total).astype(jnp.bfloat16))
    return jnp.concatenate(pieces_out, axis=0)


def shards(queries, key_heads, value_tensor, distance_use, block_pick):
    query_count = queries.shape[0]
    kv_count = key_heads.shape[0]
    query_group_width = query_count // kv_count
    token_count = queries.shape[1]
    head_width = queries.shape[2]
    number_of_blocks = token_count // BLOCK_TOKENS
    ctx_devices = lax.axis_size("ctx")
    level_count = ctx_devices.bit_length() - 1
    position = lax.axis_index("ctx")
    key_value = jnp.stack([key_heads, value_tensor])
    arrived = []
    carried = key_value
    for level_index in range(level_count):
        stride = 1 if level_index == 0 else 2 ** (level_index - 1)
        carried = from_behind(carried, "ctx", stride)
        arrived.append(carried)
    picked = []
    for level_index in range(level_count):
        shaped = arrived[level_index].reshape(
            2, kv_count, number_of_blocks, BLOCK_TOKENS, head_width
        )
        picked.append(jnp.take(shaped, block_pick[:, level_index], axis=2))
    far_pairs = jnp.stack(picked, axis=3).reshape(
        2, kv_count, number_of_blocks, level_count * BLOCK_TOKENS, head_width
    )
    strides = jnp.array([2**step_index for step_index in range(level_count)], jnp.int32)
    level_live = (distance_use[0] == 1) & (position >= strides)
    far_live = jnp.repeat(level_live, BLOCK_TOKENS)

    def one_head(head_index):
        key_value_index = head_index // query_group_width
        query_matrix = lax.dynamic_index_in_dim(queries, head_index, 0, False)
        key_local = lax.dynamic_index_in_dim(key_heads, key_value_index, 0, False)
        value_local = lax.dynamic_index_in_dim(value_tensor, key_value_index, 0, False)
        remote_key = lax.dynamic_index_in_dim(far_pairs[0], key_value_index, 0, False)
        remote_value = lax.dynamic_index_in_dim(far_pairs[1], key_value_index, 0, False)
        return attend(query_matrix, key_local, value_local, remote_key, remote_value, far_live)

    outputs = lax.map(one_head, jnp.arange(query_count, dtype=jnp.int32))
    result = jax.tree.map(
        lambda part, own: part.astype(own.dtype),
        lax.all_to_all(for_sending(outputs), "head", split_axis=1, concat_axis=0, tiled=True),
        outputs,
    )
    return result


def solution(mesh):
    placed = (
        P("head", "ctx", None),
        P("head", "ctx", None),
        P("head", "ctx", None),
        P("ctx", None),
        P("ctx", None),
    )
    return jax.shard_map(
        shards,
        mesh=mesh,
        in_specs=placed,
        out_specs=P(None, ("ctx", "head"), None),
        check_vma=False,
    )
```

profile of v0, /device:TPU:193, one launch (start us, length us, event | category | flops | bytes accessed | tf_op | source)
XLA Modules:
  0.0 208.8 jit_solution(12343487573954359473)
XLA Ops:
  0.0 1.1 pad_maximum_fusion
  1.1 3.2 %collective-permute-start = (bf16[2,1,1024,128]{3,2,1,0:T(8,128)(2,1)S(1)}, bf16[2,1,1024,128]{3,2,1,0:T(8,128)(2,1)S(1)}, u32[]{:S(2)}, u32[]{:S(2)}) collective-permute-start(bf16[2,1,1024,128]{3,2,1,0:T(8,128)(2,1)S(1)} %pad_maximum_fusion), channel_id=1, source_target_pairs={{0,8},{8,16},{16,24},{24,32},{32,40},{40,48},{48,56},{56,64},{64,7... | collective-permute-start | bytes 1572872 | tf_op jit(solution)/shard_map/ppermute | solution.py:14
  4.3 1.1 slice_reduce_fusion
  5.5 12.4 %collective-permute-done = bf16[2,1,1024,128]{3,2,1,0:T(8,128)(2,1)S(1)} collective-permute-done((bf16[2,1,1024,128]{3,2,1,0:T(8,128)(2,1)S(1)}, bf16[2,1,1024,128]{3,2,1,0:T(8,128)(2,1)S(1)}, u32[]{:S(2)}, u32[]{:S(2)}) %collective-permute-start) | collective-permute-done | bytes 524320 | tf_op jit(solution)/shard_map/ppermute | solution.py:14
  17.9 1.9 collective-permute-start.1
  19.8 13.9 %collective-permute-done.1 = bf16[2,1,1024,128]{3,2,1,0:T(8,128)(2,1)S(1)} collective-permute-done((bf16[2,1,1024,128]{3,2,1,0:T(8,128)(2,1)S(1)}, bf16[2,1,1024,128]{3,2,1,0:T(8,128)(2,1)S(1)}, u32[]{:S(2)}, u32[]{:S(2)}) %collective-permute-start.1) | collective-permute-done | bytes 524320 | tf_op jit(solution)/shard_map/ppermute | solution.py:14
  33.7 1.9 collective-permute-start.2
  35.7 13.3 %collective-permute-done.2 = bf16[2,1,1024,128]{3,2,1,0:T(8,128)(2,1)S(1)} collective-permute-done((bf16[2,1,1024,128]{3,2,1,0:T(8,128)(2,1)S(1)}, bf16[2,1,1024,128]{3,2,1,0:T(8,128)(2,1)S(1)}, u32[]{:S(2)}, u32[]{:S(2)}) %collective-permute-start.2) | collective-permute-done | bytes 524320 | tf_op jit(solution)/shard_map/ppermute | solution.py:14
  49.0 2.6 %collective-permute-start.3 = (bf16[2,1,1024,128]{3,2,1,0:T(8,128)(2,1)S(1)}, bf16[2,1,1024,128]{3,2,1,0:T(8,128)(2,1)S(1)}, u32[]{:S(2)}, u32[]{:S(2)}) collective-permute-start(bf16[2,1,1024,128]{3,2,1,0:T(8,128)(2,1)S(1)} %collective-permute-done.2), channel_id=1, source_target_pairs={{0,32},{8,40},{16,48},{24,56},{32,64},{40,72},{48,80},{56,88},{64,... | collective-permute-start | bytes 1572872 | tf_op jit(solution)/shard_map/ppermute | solution.py:14
  53.0 1.0 fusion.53
  54.6 6.3 %collective-permute-done.3 = bf16[2,1,1024,128]{3,2,1,0:T(8,128)(2,1)S(1)} collective-permute-done((bf16[2,1,1024,128]{3,2,1,0:T(8,128)(2,1)S(1)}, bf16[2,1,1024,128]{3,2,1,0:T(8,128)(2,1)S(1)}, u32[]{:S(2)}, u32[]{:S(2)}) %collective-permute-start.3) | collective-permute-done | bytes 524320 | tf_op jit(solution)/shard_map/ppermute | solution.py:14
  60.9 1.3 collective-permute-start.4
  62.2 1.0 fusion.51
  63.8 1.0 fusion.49
  65.5 1.0 fusion.47
  66.5 23.8 %collective-permute-done.4 = bf16[2,1,1024,128]{3,2,1,0:T(8,128)(2,1)S(1)} collective-permute-done((bf16[2,1,1024,128]{3,2,1,0:T(8,128)(2,1)S(1)}, bf16[2,1,1024,128]{3,2,1,0:T(8,128)(2,1)S(1)}, u32[]{:S(2)}, u32[]{:S(2)}) %collective-permute-start.4) | collective-permute-done | bytes 524320 | tf_op jit(solution)/shard_map/ppermute | solution.py:14
  91.0 1.0 fusion.45
  92.0 2.0 copy.12
  94.0 76.7 %while.11 = (s32[]{:T(128)}, bf16[8,1024,128]{2,1,0:T(8,128)(2,1)}, s32[8]{0:T(128)S(1)}, bf16[8,1024,128]{2,1,0:T(8,128)(2,1)}, bf16[1,1024,128]{2,1,0:T(8,128)...) while((s32[]{:T(128)}, bf16[8,1024,128]{2,1,0:T(8,128)(2,1)}, ...), condition=%wide.region_9.11_spmd.clone, body=%wide.region_0.10_spmd.clone.sunk | while | flops 749993472 | bytes 23674172 | solution.py:118
  96.7 1.0 constant_dynamic-slice_fusion.3
  102.9 0.7 fusion.105
  106.3 1.0 constant_dynamic-slice_fusion.3
  112.4 0.7 fusion.105
  115.9 1.0 constant_dynamic-slice_fusion.3
  125.5 1.0 constant_dynamic-slice_fusion.3
  135.1 1.0 constant_dynamic-slice_fusion.3
  144.7 1.0 constant_dynamic-slice_fusion.3
  154.2 1.0 constant_dynamic-slice_fusion.3
  163.8 1.0 constant_dynamic-slice_fusion.3
  170.7 2.9 %copy.14 = bf16[8,1024,128]{2,0,1:T(8,128)(2,1)S(1)} copy(bf16[8,1024,128]{2,1,0:T(8,128)(2,1)} %get-tuple-element.48) | data formatting | bytes 4194304 | tf_op jit(solution)/shard_map/while | solution.py:118
  173.6 33.2 %all_to_all.18 = bf16[8,1024,128]{2,0,1:T(8,128)(2,1)S(1)} all-to-all(bf16[8,1024,128]{2,0,1:T(8,128)(2,1)S(1)} %copy.14), channel_id=1, replica_groups=mesh['ctx'=32,'head'=8] {'head'}, dimensions={1} | all-to-all | bytes 4194304 | tf_op jit(solution)/shard_map/all_to_all | solution.py:121
  206.9 1.9 copy.15
  (201 shorter events, 54.2 us)
Async XLA Ops:
  1.1 16.8 %collective-permute-start = (bf16[2,1,1024,128]{3,2,1,0:T(8,128)(2,1)S(1)}, bf16[2,1,1024,128]{3,2,1,0:T(8,128)(2,1)S(1)}, u32[]{:S(2)}, u32[]{:S(2)}) collective-permute-start(bf16[2,1,1024,128]{3,2,1,0:T(8,128)(2,1)S(1)} %pad_maximum_fusion), channel_id=1, source_target_pairs={{0,8},{8,16},{16,24},{24,32},{32,40},{40,48},{48,56},{56,64},{64,7... | collective-permute-start | bytes 1572872 | tf_op jit(solution)/shard_map/ppermute | solution.py:14
  17.9 15.9 %collective-permute-start.1 = (bf16[2,1,1024,128]{3,2,1,0:T(8,128)(2,1)S(1)}, bf16[2,1,1024,128]{3,2,1,0:T(8,128)(2,1)S(1)}, u32[]{:S(2)}, u32[]{:S(2)}) collective-permute-start(bf16[2,1,1024,128]{3,2,1,0:T(8,128)(2,1)S(1)} %collective-permute-done), channel_id=1, source_target_pairs={{0,8},{8,16},{16,24},{24,32},{32,40},{40,48},{48,56},{56,64},{64,7... | collective-permute-start | bytes 1572872 | tf_op jit(solution)/shard_map/ppermute | solution.py:14
  33.7 15.2 %collective-permute-start.2 = (bf16[2,1,1024,128]{3,2,1,0:T(8,128)(2,1)S(1)}, bf16[2,1,1024,128]{3,2,1,0:T(8,128)(2,1)S(1)}, u32[]{:S(2)}, u32[]{:S(2)}) collective-permute-start(bf16[2,1,1024,128]{3,2,1,0:T(8,128)(2,1)S(1)} %collective-permute-done.1), channel_id=1, source_target_pairs={{0,16},{8,24},{16,32},{24,40},{32,48},{40,56},{48,64},{56,72},{64,... | collective-permute-start | bytes 1572872 | tf_op jit(solution)/shard_map/ppermute | solution.py:14
  49.0 11.9 %collective-permute-start.3 = (bf16[2,1,1024,128]{3,2,1,0:T(8,128)(2,1)S(1)}, bf16[2,1,1024,128]{3,2,1,0:T(8,128)(2,1)S(1)}, u32[]{:S(2)}, u32[]{:S(2)}) collective-permute-start(bf16[2,1,1024,128]{3,2,1,0:T(8,128)(2,1)S(1)} %collective-permute-done.2), channel_id=1, source_target_pairs={{0,32},{8,40},{16,48},{24,56},{32,64},{40,72},{48,80},{56,88},{64,... | collective-permute-start | bytes 1572872 | tf_op jit(solution)/shard_map/ppermute | solution.py:14
  60.9 29.4 %collective-permute-start.4 = (bf16[2,1,1024,128]{3,2,1,0:T(8,128)(2,1)S(1)}, bf16[2,1,1024,128]{3,2,1,0:T(8,128)(2,1)S(1)}, u32[]{:S(2)}, u32[]{:S(2)}) collective-permute-start(bf16[2,1,1024,128]{3,2,1,0:T(8,128)(2,1)S(1)} %collective-permute-done.3), channel_id=1, source_target_pairs={{0,64},{8,72},{16,80},{24,88},{32,96},{40,104},{48,112},{56,120},{... | collective-permute-start | bytes 1572872 | tf_op jit(solution)/shard_map/ppermute | solution.py:14
  92.0 2.0 copy-start
  92.0 2.0 copy-start.1
where the time goes:
time: 212 us; the launch traced here: 209 us
  waiting for transfers between devices  69.6 us (33%)
  blocking collectives  33.2 us (16%)
  matrix products  27.9 us (13%)
  local copies, waits for them, and re-layouts  25 us (12%)
  other arithmetic  24.7 us (12%)
  loops' own time  17.1 us (8%)
  starting transfers between devices  10.9 us (5%)
    ppermute x5, waiting for transfers between devices, from_behind(): lax.ppermute(value, axis, [(source, source + steps) for source in range(i...  69.6 us
    all_to_all x1, blocking collectives, shards(): lax.all_to_all(for_sending(outputs), 'head', split_axis=1, concat_axis=0,...  33.2 us
    another operation x1, loops' own time, shards(): outputs = lax.map(one_head, jnp.arange(query_count, dtype=jnp.int32))  17.1 us
    ppermute x5, starting transfers between devices, from_behind(): lax.ppermute(value, axis, [(source, source + steps) for source in range(i...  10.9 us
    slice x8, local copies, waits for them, and re-layouts, attend(): rows_now = query_matrix[first_row:last_row]  7.94 us
    dot_general x16, matrix products, attend(): jnp.einsum('ghj,gcj->ghc', rows_of_block, current_remote_keys, preferred_...  7.33 us
    dot_general x16, matrix products, attend(): jnp.einsum('qd,kd->qk', rows_now, key_local[:last_row], preferred_element...  7.17 us
    dot_general x16, matrix products, attend(): jnp.dot(near_weights.astype(jnp.bfloat16), value_local[:last_row], prefer...  7.04 us
  transfers between devices with their start and end apart: 5, of which 5 were waited for; matrix products, arithmetic and copies ran while one was open for 4% of the time, Pallas kernels for 0%

commit v1 on v0

v1 whole, which is shorter than its diff:
```python
import functools
import math

import jax
import jax.numpy as jnp
from jax import lax
from jax.experimental import pallas as pl
from jax.experimental.pallas import tpu as pltpu
from jax.sharding import PartitionSpec as P

BLOCK = 128
LEVELS = 5
Y_COUNT = 4
FORWARD_BLOCKS = 3
Y1, Y2, Z1, Z2, Z4F, RELAY, Z4B = range(7)
EXCHANGE_ORDER = (4, 3, 5, 2, 6, 1, 7)


def kernel(
    q_hbm, k_ref, v_ref, use_ref, pick_ref, out_ref,
    q_ref, far_keys, far_values, relay_ref, total_ref, inverse_ref, weight_ref, made_ref,
    send_sem, recv_sem, out_send_sem, out_recv_sem, own_sem,
):
    heads, tokens, width = q_ref.shape
    blocks = tokens // BLOCK
    ctx = lax.axis_index("ctx")
    head = lax.axis_index("head")
    shards = lax.axis_size("ctx")
    head_devices = lax.axis_size("head")
    z = ctx // Y_COUNT
    y = ctx % Y_COUNT
    along_z = lambda steps: lax.rem(ctx + (steps * Y_COUNT) % shards, shards)
    along_y = lambda steps: z * Y_COUNT + lax.rem(y + steps % Y_COUNT, Y_COUNT)

    take_queries = pltpu.make_async_copy(q_hbm, q_ref, own_sem.at[0])
    take_queries.start()

    barrier = pltpu.get_barrier_semaphore()
    ctx_peers = [along_z(s) for s in (1, -1, 2, -2, 3, -3)] + [along_y(s) for s in (1, -1, 2)]
    for peer in ctx_peers:
        pl.semaphore_signal(barrier, inc=1, device_id={"ctx": peer}, device_id_type=pl.DeviceIdType.MESH)
    for step in range(1, head_devices):
        pl.semaphore_signal(
            barrier, inc=1, device_id={"head": lax.rem(head + step, head_devices)},
            device_id_type=pl.DeviceIdType.MESH,
        )
    pl.semaphore_wait(barrier, len(ctx_peers) + head_devices - 1)

    own = (k_ref.at[0], v_ref.at[0])
    far = (far_keys, far_values)
    top = pl.ds(0, FORWARD_BLOCKS)
    rest = pl.ds(FORWARD_BLOCKS, blocks - FORWARD_BLOCKS)

    def copy(kind, lane, source, target, peer):
        return pltpu.make_async_remote_copy(
            src_ref=source, dst_ref=target,
            send_sem=send_sem.at[kind, lane], recv_sem=recv_sem.at[kind, lane],
            device_id={"ctx": peer}, device_id_type=pl.DeviceIdType.MESH,
        )

    def near_y1(t): return copy(t, Y1, own[t], far[t].at[0], along_y(1))
    def wrap_y1(t): return copy(t, Y1, far[t].at[2], far[t].at[0], along_y(1))
    def near_y2(t): return copy(t, Y2, own[t], far[t].at[1], along_y(2))
    def wrap_y2(t): return copy(t, Y2, far[t].at[2], far[t].at[1], along_y(2))
    def hop_z1(t): return copy(t, Z1, own[t], far[t].at[2], along_z(1))
    def hop_z2(t): return copy(t, Z2, far[t].at[2], far[t].at[3], along_z(1))
    def hop_z4f(t): return copy(t, Z4F, far[t].at[3, top], far[t].at[4, top], along_z(2))
    def hop_relay(t): return copy(t, RELAY, own[t].at[rest], relay_ref.at[t], along_z(-3))
    def hop_z4b(t): return copy(t, Z4B, relay_ref.at[t], far[t].at[4, rest], along_z(-1))

    relays = (z >= 5) | (z == 0)
    forwards = (z >= 2) & (z <= 5)

    def first(t):
        pl.when(z < 7)(lambda: hop_z1(t).start())
        pl.when(z < 4)(lambda: hop_relay(t).start())
        pl.when(y < 3)(lambda: near_y1(t).start())
        pl.when(y < 2)(lambda: near_y2(t).start())

    def second(t):
        @pl.when(z >= 1)
        def _():
            hop_z1(t).wait_recv()
            pl.when(z <= 6)(lambda: hop_z2(t).start())
            pl.when(y == 3)(lambda: wrap_y1(t).start())
            pl.when(y >= 2)(lambda: wrap_y2(t).start())

    def third(t):
        pl.when(z >= 2)(lambda: hop_z2(t).wait_recv())
        pl.when(forwards)(lambda: hop_z4f(t).start())

    def fourth(t):
        @pl.when(relays)
        def _():
            hop_relay(t).wait_recv()
            hop_z4b(t).start()

    def last(t):
        pl.when(ctx >= 1)(lambda: near_y1(t).wait_recv())
        pl.when(ctx >= 2)(lambda: near_y2(t).wait_recv())

        @pl.when(z >= 4)
        def _():
            hop_z4f(t).wait_recv()
            hop_z4b(t).wait_recv()

    def all_sent(t):
        pl.when(z < 7)(lambda: hop_z1(t).wait_send())
        pl.when(z < 4)(lambda: hop_relay(t).wait_send())
        pl.when((y < 3) | (z >= 1))(lambda: near_y1(t).wait_send())
        pl.when((y < 2) | (z >= 1))(lambda: near_y2(t).wait_send())
        pl.when((z >= 1) & (z <= 6))(lambda: hop_z2(t).wait_send())
        pl.when(forwards)(lambda: hop_z4f(t).wait_send())
        pl.when(relays)(lambda: hop_z4b(t).wait_send())

    first(0)
    for level in range(LEVELS):
        @pl.when(ctx < 2**level)
        def _(level=level):
            nothing = jnp.zeros((blocks, BLOCK, width), far_keys.dtype)
            far_keys[level] = nothing
            far_values[level] = nothing

    take_queries.wait()
    second(0)
    third(0)
    fourth(0)
    first(1)
    last(0)

    def picked(t, block):
        return jnp.concatenate(
            [far[t][level, pick_ref[block, level]] for level in range(LEVELS)], axis=0
        )

    exponent_scale = math.log2(math.e) / math.sqrt(width)
    bias = []
    for level in range(LEVELS):
        live = use_ref[0, level] * jnp.where(ctx >= 2**level, 1, 0)
        bias.append(jnp.full((1, BLOCK), (live.astype(jnp.float32) - 1.0) * 3e38, jnp.float32))
    bias = jnp.concatenate(bias, axis=1)
    rows = 2 * BLOCK

    def score_group(group):
        before = group * 2 * BLOCK
        near_width = before + 2 * BLOCK

        def body(step, carry):
            in_group = step // 4
            block = group * 2 + in_group
            pair = step % 4
            first_row = pl.multiple_of(block * BLOCK, BLOCK)
            row_slice = pl.ds(pl.multiple_of(pair * rows, rows), rows)
            q_now = q_ref[pl.ds(pair * 2, 2), pl.ds(first_row, BLOCK), :].reshape(rows, width)
            keys = jnp.concatenate([k_ref[0, : near_width // BLOCK].reshape(near_width, width), picked(0, block)], axis=0)
            scores = lax.dot_general(
                q_now, keys, (((1,), (1,)), ((), ())), preferred_element_type=jnp.float32
            )
            row_pos = lax.broadcasted_iota(jnp.int32, (rows, rows), 0) % BLOCK + in_group * BLOCK
            col_pos = lax.broadcasted_iota(jnp.int32, (rows, rows), 1)
            diagonal = jnp.where(col_pos <= row_pos, scores[:, before:near_width], -jnp.inf)
            distant = scores[:, near_width:] + bias
            parts = [scores[:, :before]] if group else []
            scores = jnp.concatenate(parts + [diagonal, distant], axis=1)
            peak = jnp.max(scores, axis=1, keepdims=True)
            weights = jnp.exp2((scores - peak) * exponent_scale)
            row_total = jnp.sum(weights, axis=1, keepdims=True)
            rounded = weights.astype(jnp.bfloat16)
            weight_ref[block, row_slice, :] = rounded[:, near_width:]
            total_ref[block, row_slice, :] = jnp.dot(
                rounded[:, :near_width], v_ref[0, : near_width // BLOCK].reshape(near_width, width), preferred_element_type=jnp.float32
            )
            inverse_ref[block, row_slice, :] = jnp.broadcast_to(1.0 / row_total, (rows, width))
            return carry

        lax.fori_loop(0, 8, body, 0)

    score_group(0)
    second(1)
    score_group(1)
    score_group(2)
    third(1)
    fourth(1)
    score_group(3)
    last(1)

    mine = pl.ds(head * heads, heads)

    def make(step):
        block = lax.rem(head + step, head_devices)
        values = picked(1, block)

        def body(pair, carry):
            row_slice = pl.ds(pl.multiple_of(pair * rows, rows), rows)
            distant = jnp.dot(weight_ref[block, row_slice, :], values, preferred_element_type=jnp.float32)
            result = (total_ref[block, row_slice, :] + distant) * inverse_ref[block, row_slice, :]
            made_ref[step, pl.ds(pair * 2, 2)] = result.astype(made_ref.dtype).reshape(2, BLOCK, width)
            return carry

        lax.fori_loop(0, heads // 2, body, 0)

    def give(step):
        return pltpu.make_async_remote_copy(
            src_ref=made_ref.at[step], dst_ref=out_ref.at[mine],
            send_sem=out_send_sem.at[step], recv_sem=out_recv_sem.at[step],
            device_id={"head": lax.rem(head + step, head_devices)},
            device_id_type=pl.DeviceIdType.MESH,
        )

    for place, step in enumerate(EXCHANGE_ORDER):
        make(step)
        if place:
            give(EXCHANGE_ORDER[place - 1]).start()
    make(0)
    give(EXCHANGE_ORDER[-1]).start()
    keep = pltpu.make_async_copy(made_ref.at[0], out_ref.at[mine], own_sem.at[1])
    keep.start()
    all_sent(0)
    all_sent(1)
    keep.wait()
    for step in EXCHANGE_ORDER:
        give(step).wait()


def shards(queries, key_heads, value_tensor, distance_use, block_pick):
    heads, tokens, width = queries.shape
    blocks = tokens // BLOCK
    head_devices = lax.axis_size("head")
    vmem = pl.BlockSpec(memory_space=pltpu.VMEM)
    smem = pl.BlockSpec(memory_space=pltpu.SMEM)
    anywhere = pl.BlockSpec(memory_space=pl.ANY)
    return pl.pallas_call(
        kernel,
        out_shape=jax.ShapeDtypeStruct((heads * head_devices, tokens // head_devices, width), queries.dtype),
        in_specs=[anywhere, vmem, vmem, smem, smem],
        out_specs=anywhere,
        scratch_shapes=[
            pltpu.VMEM((heads, tokens, width), jnp.bfloat16),
            pltpu.VMEM((LEVELS, blocks, BLOCK, width), jnp.bfloat16),
            pltpu.VMEM((LEVELS, blocks, BLOCK, width), jnp.bfloat16),
            pltpu.VMEM((2, blocks - FORWARD_BLOCKS, BLOCK, width), jnp.bfloat16),
            pltpu.VMEM((blocks, heads * BLOCK, width), jnp.float32),
            pltpu.VMEM((blocks, heads * BLOCK, width), jnp.float32),
            pltpu.VMEM((blocks, heads * BLOCK, LEVELS * BLOCK), jnp.bfloat16),
            pltpu.VMEM((blocks, heads, BLOCK, width), jnp.bfloat16),
            pltpu.SemaphoreType.DMA((2, 7)),
            pltpu.SemaphoreType.DMA((2, 7)),
            pltpu.SemaphoreType.DMA((8,)),
            pltpu.SemaphoreType.DMA((8,)),
            pltpu.SemaphoreType.DMA((2,)),
        ],
        compiler_params=pltpu.CompilerParams(
            collective_id=0, has_side_effects=True, vmem_limit_bytes=60 * 1024 * 1024
        ),
        name="power_attention",
    )(
        queries,
        key_heads.reshape(1, blocks, BLOCK, width),
        value_tensor.reshape(1, blocks, BLOCK, width),
        distance_use,
        block_pick,
    )


def solution(mesh):
    placed = (
        P("head", "ctx", None),
        P("head", "ctx", None),
        P("head", "ctx", None),
        P("ctx", None),
        P("ctx", None),
    )
    return jax.shard_map(
        shards,
        mesh=mesh,
        in_specs=placed,
        out_specs=P(None, ("ctx", "head"), None),
        check_vma=False,
    )
```

time: 212 us -> 85.8 us (0.40)
  the two profiles are of different devices: /device:TPU:193 before, /device:TPU:32 now
where the time goes in v1:
time: 85.8 us; the launch traced here: 85.7 us
  Pallas kernels  82.5 us (96%)
  local copies, waits for them, and re-layouts  3.16 us (4%)
    pallas_call x1, Pallas kernels, shards(): pl.pallas_call(kernel, out_shape=jax.ShapeDtypeStruct((heads * head_devic...  82.5 us
    unnamed x1, local copies, waits for them, and re-layouts  3.16 us

profile of v1, /device:TPU:32, one launch (start us, length us, event | category | flops | bytes accessed | tf_op | source)
XLA Modules:
  0.0 85.7 jit_solution(4523160090490967625)
XLA Ops:
  0.0 82.5 %power_attention.1 = bf16[64,128,128]{2,1,0:T(8,128)(2,1)} custom-call(bf16[8,1024,128]{2,1,0:T(8,128)(2,1)} %q_hbm.1, bf16[1,8,128,128]{3,2,1,0:T(8,128)(2,1)} %bitcast.2, bf16[1,8,128,128]{3,2,1,0:T(8,128)(2,1)} %bitcast.3, s32[1,5]{1,0:T(1,128)} %use_ref.1, s32[8,5]{1,0:T(8,128)} %pick_ref.1), custom_call_target="tpu_custom_call" | custom-call | tf_op jit(solution)/shard_map/power_attention/pallas_call | solution.py:232
  82.5 3.2 %copy.7 = bf16[64,128,128]{2,1,0:T(8,128)(2,1)} copy(bf16[64,128,128]{2,1,0:T(8,128)(2,1)} %power_attention.1) | data formatting | bytes 4194304

commit v2 on v1

--- a/solution.py
+++ b/solution.py
@@ -12,13 +12,14 @@
 LEVELS = 5
 Y_COUNT = 4
 FORWARD_BLOCKS = 3
-Y1, Y2, Z1, Z2, Z4F, RELAY, Z4B = range(7)
-EXCHANGE_ORDER = (4, 3, 5, 2, 6, 1, 7)
+Y1, Y2, Z1, Z2, Z4F, RELAY, Z4B, Y_RELAY, Y2_BACK = range(9)
+X_COUNT = 4
+DIRECT, SIBLING, LEG1, LEG2 = 0, 4, 5, 9
 
 
 def kernel(
     q_hbm, k_ref, v_ref, use_ref, pick_ref, out_ref,
-    q_ref, far_keys, far_values, relay_ref, total_ref, inverse_ref, weight_ref, made_ref,
+    q_ref, far_keys, far_values, relay_ref, y_relay_ref, total_ref, inverse_ref, weight_ref, made_ref, passing_ref,
     send_sem, recv_sem, out_send_sem, out_recv_sem, own_sem,
 ):
     heads, tokens, width = q_ref.shape
@@ -36,7 +37,7 @@
     take_queries.start()
 
     barrier = pltpu.get_barrier_semaphore()
-    ctx_peers = [along_z(s) for s in (1, -1, 2, -2, 3, -3)] + [along_y(s) for s in (1, -1, 2)]
+    ctx_peers = [along_z(s) for s in (1, -1, 2, -2, 3, -3)] + [along_y(s) for s in (1, -1)]
     for peer in ctx_peers:
         pl.semaphore_signal(barrier, inc=1, device_id={"ctx": peer}, device_id_type=pl.DeviceIdType.MESH)
     for step in range(1, head_devices):
@@ -60,8 +61,9 @@
 
     def near_y1(t): return copy(t, Y1, own[t], far[t].at[0], along_y(1))
     def wrap_y1(t): return copy(t, Y1, far[t].at[2], far[t].at[0], along_y(1))
-    def near_y2(t): return copy(t, Y2, own[t], far[t].at[1], along_y(2))
-    def wrap_y2(t): return copy(t, Y2, far[t].at[2], far[t].at[1], along_y(2))
+    def forward_y2(t): return copy(t, Y2, far[t].at[0], far[t].at[1], along_y(1))
+    def hop_y_relay(t): return copy(t, Y_RELAY, far[t].at[2], y_relay_ref.at[t], along_y(-1))
+    def back_y2(t): return copy(t, Y2_BACK, y_relay_ref.at[t], far[t].at[1], along_y(-1))
     def hop_z1(t): return copy(t, Z1, own[t], far[t].at[2], along_z(1))
     def hop_z2(t): return copy(t, Z2, far[t].at[2], far[t].at[3], along_z(1))
     def hop_z4f(t): return copy(t, Z4F, far[t].at[3, top], far[t].at[4, top], along_z(2))
@@ -75,7 +77,6 @@
         pl.when(z < 7)(lambda: hop_z1(t).start())
         pl.when(z < 4)(lambda: hop_relay(t).start())
         pl.when(y < 3)(lambda: near_y1(t).start())
-        pl.when(y < 2)(lambda: near_y2(t).start())
 
     def second(t):
         @pl.when(z >= 1)
@@ -83,21 +84,37 @@
             hop_z1(t).wait_recv()
             pl.when(z <= 6)(lambda: hop_z2(t).start())
             pl.when(y == 3)(lambda: wrap_y1(t).start())
-            pl.when(y >= 2)(lambda: wrap_y2(t).start())
+            pl.when(y == 2)(lambda: hop_y_relay(t).start())
+
+        @pl.when((y == 1) | (y == 2))
+        def _():
+            near_y1(t).wait_recv()
+            forward_y2(t).start()
 
     def third(t):
         pl.when(z >= 2)(lambda: hop_z2(t).wait_recv())
         pl.when(forwards)(lambda: hop_z4f(t).start())
 
     def fourth(t):
+        @pl.when((y == 0) & (z >= 1))
+        def _():
+            near_y1(t).wait_recv()
+            forward_y2(t).start()
+
+        @pl.when((y == 1) & (z >= 1))
+        def _():
+            hop_y_relay(t).wait_recv()
+            back_y2(t).start()
+
         @pl.when(relays)
         def _():
             hop_relay(t).wait_recv()
             hop_z4b(t).start()
 
     def last(t):
-        pl.when(ctx >= 1)(lambda: near_y1(t).wait_recv())
-        pl.when(ctx >= 2)(lambda: near_y2(t).wait_recv())
+        pl.when(y == 3)(lambda: near_y1(t).wait_recv())
+        pl.when((y >= 2) | ((y == 1) & (z >= 1)))(lambda: forward_y2(t).wait_recv())
+        pl.when((y == 0) & (z >= 1))(lambda: back_y2(t).wait_recv())
 
         @pl.when(z >= 4)
         def _():
@@ -108,7 +125,9 @@
         pl.when(z < 7)(lambda: hop_z1(t).wait_send())
         pl.when(z < 4)(lambda: hop_relay(t).wait_send())
         pl.when((y < 3) | (z >= 1))(lambda: near_y1(t).wait_send())
-        pl.when((y < 2) | (z >= 1))(lambda: near_y2(t).wait_send())
+        pl.when((y == 1) | (y == 2) | ((y == 0) & (z >= 1)))(lambda: forward_y2(t).wait_send())
+        pl.when((y == 2) & (z >= 1))(lambda: hop_y_relay(t).wait_send())
+        pl.when((y == 1) & (z >= 1))(lambda: back_y2(t).wait_send())
         pl.when((z >= 1) & (z <= 6))(lambda: hop_z2(t).wait_send())
         pl.when(forwards)(lambda: hop_z4f(t).wait_send())
         pl.when(relays)(lambda: hop_z4b(t).wait_send())
@@ -184,42 +203,81 @@
     score_group(3)
     last(1)
 
-    mine = pl.ds(head * heads, heads)
-
-    def make(step):
-        block = lax.rem(head + step, head_devices)
+    x = head // 2
+    core = head % 2
+    half = heads // 2
+
+    def device(x_steps, to_core):
+        return lax.rem(x + x_steps, X_COUNT) * 2 + to_core
+
+    targets = [device(2, 0), device(2, 1), device(1, 0), device(3, 0), device(1, 1), device(3, 1), device(0, 1 - core), head]
+
+    def make(slot):
+        block = targets[slot]
         values = picked(1, block)
 
         def body(pair, carry):
             row_slice = pl.ds(pl.multiple_of(pair * rows, rows), rows)
             distant = jnp.dot(weight_ref[block, row_slice, :], values, preferred_element_type=jnp.float32)
             result = (total_ref[block, row_slice, :] + distant) * inverse_ref[block, row_slice, :]
-            made_ref[step, pl.ds(pair * 2, 2)] = result.astype(made_ref.dtype).reshape(2, BLOCK, width)
+            made_ref[slot, pl.ds(pair * 2, 2)] = result.astype(made_ref.dtype).reshape(2, BLOCK, width)
             return carry
 
         lax.fori_loop(0, heads // 2, body, 0)
 
-    def give(step):
+    def give(source, target, sent, received, to_head):
         return pltpu.make_async_remote_copy(
-            src_ref=made_ref.at[step], dst_ref=out_ref.at[mine],
-            send_sem=out_send_sem.at[step], recv_sem=out_recv_sem.at[step],
-            device_id={"head": lax.rem(head + step, head_devices)},
-            device_id_type=pl.DeviceIdType.MESH,
-        )
-
-    for place, step in enumerate(EXCHANGE_ORDER):
-        make(step)
-        if place:
-            give(EXCHANGE_ORDER[place - 1]).start()
-    make(0)
-    give(EXCHANGE_ORDER[-1]).start()
-    keep = pltpu.make_async_copy(made_ref.at[0], out_ref.at[mine], own_sem.at[1])
+            src_ref=source, dst_ref=target,
+            send_sem=out_send_sem.at[sent], recv_sem=out_recv_sem.at[received],
+            device_id={"head": to_head}, device_id_type=pl.DeviceIdType.MESH,
+        )
+
+    mine = pl.ds(head * heads, heads)
+
+    def leg1(part, to_core):
+        source = made_ref.at[to_core, pl.ds(part * half, half)]
+        place = LEG1 + part * 2 + to_core
+        return give(source, passing_ref.at[part, to_core], place, place, device((1, 3)[part], core))
+
+    def leg2(part, to_core, received):
+        source_head = device((3, 1)[part], core)
+        target = out_ref.at[pl.ds(source_head * heads + part * half, half)]
+        return give(
+            passing_ref.at[part, to_core], target, LEG2 + part * 2 + to_core, received,
+            device((1, 3)[part], to_core),
+        )
+
+    def direct(slot, received):
+        return give(made_ref.at[slot], out_ref.at[mine], DIRECT + slot - 2, received, targets[slot])
+
+    def start(slot):
+        if slot < 2:
+            leg1(0, slot).start()
+            leg1(1, slot).start()
+        elif slot < 6:
+            direct(slot, DIRECT + (slot % 2) * 2 + core).start()
+        else:
+            direct(slot, SIBLING).start()
+
+    for slot in range(8):
+        make(slot)
+        if slot:
+            start(slot - 1)
+    keep = pltpu.make_async_copy(made_ref.at[7], out_ref.at[mine], own_sem.at[1])
     keep.start()
+    for part in range(2):
+        for to_core in range(2):
+            leg1(part, to_core).wait_recv()
+            leg2(part, to_core, LEG2 + part * 2 + core).start()
     all_sent(0)
     all_sent(1)
     keep.wait()
-    for step in EXCHANGE_ORDER:
-        give(step).wait()
+    for slot in range(2, 7):
+        direct(slot, DIRECT + slot - 2).wait()
+    for part in range(2):
+        for to_core in range(2):
+            leg1(part, to_core).wait_send()
+            leg2(part, to_core, LEG2 + part * 2 + to_core).wait()
 
 
 def shards(queries, key_heads, value_tensor, distance_use, block_pick):
@@ -239,14 +297,16 @@
             pltpu.VMEM((LEVELS, blocks, BLOCK, width), jnp.bfloat16),
             pltpu.VMEM((LEVELS, blocks, BLOCK, width), jnp.bfloat16),
             pltpu.VMEM((2, blocks - FORWARD_BLOCKS, BLOCK, width), jnp.bfloat16),
+            pltpu.VMEM((2, blocks, BLOCK, width), jnp.bfloat16),
             pltpu.VMEM((blocks, heads * BLOCK, width), jnp.float32),
             pltpu.VMEM((blocks, heads * BLOCK, width), jnp.float32),
             pltpu.VMEM((blocks, heads * BLOCK, LEVELS * BLOCK), jnp.bfloat16),
             pltpu.VMEM((blocks, heads, BLOCK, width), jnp.bfloat16),
-            pltpu.SemaphoreType.DMA((2, 7)),
-            pltpu.SemaphoreType.DMA((2, 7)),
-            pltpu.SemaphoreType.DMA((8,)),
-            pltpu.SemaphoreType.DMA((8,)),
+            pltpu.VMEM((2, 2, heads // 2, BLOCK, width), jnp.bfloat16),
+            pltpu.SemaphoreType.DMA((2, 9)),
+            pltpu.SemaphoreType.DMA((2, 9)),
+            pltpu.SemaphoreType.DMA((13,)),
+            pltpu.SemaphoreType.DMA((13,)),
             pltpu.SemaphoreType.DMA((2,)),
         ],
         compiler_params=pltpu.CompilerParams(

time: 85.8 us -> 84.5 us (0.985)
  the two profiles are of different devices: /device:TPU:32 before, /device:TPU:193 now
where the time goes in v2:
time: 84.5 us; the launch traced here: 84.3 us
  Pallas kernels  81.1 us (96%)
  local copies, waits for them, and re-layouts  3.16 us (4%)
    pallas_call x1, Pallas kernels, shards(): pl.pallas_call(kernel, out_shape=jax.ShapeDtypeStruct((heads * head_devic...  81.1 us
    unnamed x1, local copies, waits for them, and re-layouts  3.16 us

profile of v2, /device:TPU:193, one launch (start us, length us, event | category | flops | bytes accessed | tf_op | source)
XLA Modules:
  0.0 84.3 jit_solution(5588948422255660599)
XLA Ops:
  0.0 81.1 %power_attention.1 = bf16[64,128,128]{2,1,0:T(8,128)(2,1)} custom-call(bf16[8,1024,128]{2,1,0:T(8,128)(2,1)} %q_hbm.1, bf16[1,8,128,128]{3,2,1,0:T(8,128)(2,1)} %bitcast.2, bf16[1,8,128,128]{3,2,1,0:T(8,128)(2,1)} %bitcast.3, s32[1,5]{1,0:T(1,128)} %use_ref.1, s32[8,5]{1,0:T(8,128)} %pick_ref.1), custom_call_target="tpu_custom_call" | custom-call | tf_op jit(solution)/shard_map/power_attention/pallas_call | solution.py:290
  81.2 3.2 %copy.7 = bf16[64,128,128]{2,1,0:T(8,128)(2,1)} copy(bf16[64,128,128]{2,1,0:T(8,128)(2,1)} %power_attention.1) | data formatting | bytes 4194304

commit v3 on v2

--- a/solution.py
+++ b/solution.py
@@ -14,12 +14,15 @@
 FORWARD_BLOCKS = 3
 Y1, Y2, Z1, Z2, Z4F, RELAY, Z4B, Y_RELAY, Y2_BACK = range(9)
 X_COUNT = 4
+STEP_HEADS = 2
+UNROLL = 1
 DIRECT, SIBLING, LEG1, LEG2 = 0, 4, 5, 9
 
 
 def kernel(
     q_hbm, k_ref, v_ref, use_ref, pick_ref, out_ref,
     q_ref, far_keys, far_values, relay_ref, y_relay_ref, total_ref, inverse_ref, weight_ref, made_ref, passing_ref,
+    near_0, near_1, near_2, near_3,
     send_sem, recv_sem, out_send_sem, out_recv_sem, own_sem,
 ):
     heads, tokens, width = q_ref.shape
@@ -49,6 +52,7 @@
 
     own = (k_ref.at[0], v_ref.at[0])
     far = (far_keys, far_values)
+    near_refs = (near_0, near_1, near_2, near_3)
     top = pl.ds(0, FORWARD_BLOCKS)
     rest = pl.ds(FORWARD_BLOCKS, blocks - FORWARD_BLOCKS)
 
@@ -141,11 +145,6 @@
             far_values[level] = nothing
 
     take_queries.wait()
-    second(0)
-    third(0)
-    fourth(0)
-    first(1)
-    last(0)
 
     def picked(t, block):
         return jnp.concatenate(
@@ -159,48 +158,91 @@
         bias.append(jnp.full((1, BLOCK), (live.astype(jnp.float32) - 1.0) * 3e38, jnp.float32))
     bias = jnp.concatenate(bias, axis=1)
     rows = 2 * BLOCK
-
-    def score_group(group):
+    step_rows = STEP_HEADS * BLOCK
+    steps_per_block = heads // STEP_HEADS
+
+    def group_shape(group):
         before = group * 2 * BLOCK
-        near_width = before + 2 * BLOCK
+        return before, before + 2 * BLOCK
+
+    def place_of(step, group):
+        in_group = step // steps_per_block
+        part = step % steps_per_block
+        block = group * 2 + in_group
+        first_row = pl.multiple_of(block * BLOCK, BLOCK)
+        row_slice = pl.ds(pl.multiple_of(part * step_rows, step_rows), step_rows)
+        q_now = q_ref[pl.ds(part * STEP_HEADS, STEP_HEADS), pl.ds(first_row, BLOCK), :]
+        return in_group, block, row_slice, q_now.reshape(step_rows, width)
+
+    def lane_peak(scores):
+        return functools.reduce(
+            jnp.maximum, [scores[:, c : c + BLOCK] for c in range(0, scores.shape[1], BLOCK)]
+        )
+
+    def score_near(group):
+        before, near_width = group_shape(group)
 
         def body(step, carry):
-            in_group = step // 4
-            block = group * 2 + in_group
-            pair = step % 4
-            first_row = pl.multiple_of(block * BLOCK, BLOCK)
-            row_slice = pl.ds(pl.multiple_of(pair * rows, rows), rows)
-            q_now = q_ref[pl.ds(pair * 2, 2), pl.ds(first_row, BLOCK), :].reshape(rows, width)
-            keys = jnp.concatenate([k_ref[0, : near_width // BLOCK].reshape(near_width, width), picked(0, block)], axis=0)
+            in_group, block, row_slice, q_now = place_of(step, group)
+            keys = k_ref[0, : near_width // BLOCK].reshape(near_width, width)
             scores = lax.dot_general(
                 q_now, keys, (((1,), (1,)), ((), ())), preferred_element_type=jnp.float32
             )
-            row_pos = lax.broadcasted_iota(jnp.int32, (rows, rows), 0) % BLOCK + in_group * BLOCK
-            col_pos = lax.broadcasted_iota(jnp.int32, (rows, rows), 1)
-            diagonal = jnp.where(col_pos <= row_pos, scores[:, before:near_width], -jnp.inf)
-            distant = scores[:, near_width:] + bias
+            row_pos = lax.broadcasted_iota(jnp.int32, (step_rows, rows), 0) % BLOCK + in_group * BLOCK
+            col_pos = lax.broadcasted_iota(jnp.int32, (step_rows, rows), 1)
+            diagonal = jnp.where(col_pos <= row_pos, scores[:, before:], -jnp.inf)
             parts = [scores[:, :before]] if group else []
-            scores = jnp.concatenate(parts + [diagonal, distant], axis=1)
-            peak = jnp.max(scores, axis=1, keepdims=True)
-            weights = jnp.exp2((scores - peak) * exponent_scale)
-            row_total = jnp.sum(weights, axis=1, keepdims=True)
-            rounded = weights.astype(jnp.bfloat16)
-            weight_ref[block, row_slice, :] = rounded[:, near_width:]
+            scores = jnp.concatenate(parts + [diagonal], axis=1)
+            near_refs[group][in_group, row_slice, :] = scores
+            inverse_ref[block, row_slice, :] = lane_peak(scores)
+            return carry
+
+        lax.fori_loop(0, 2 * steps_per_block, body, 0, unroll=UNROLL)
+
+    def score_far(group):
+        _, near_width = group_shape(group)
+
+        def body(step, carry):
+            in_group, block, row_slice, q_now = place_of(step, group)
+            distant = lax.dot_general(
+                q_now, picked(0, block), (((1,), (1,)), ((), ())), preferred_element_type=jnp.float32
+            ) + bias
+            peak = jnp.max(
+                jnp.maximum(inverse_ref[block, row_slice, :], lane_peak(distant)), axis=1, keepdims=True
+            )
+            near_weights = jnp.exp2((near_refs[group][in_group, row_slice, :] - peak) * exponent_scale)
+            far_weights = jnp.exp2((distant - peak) * exponent_scale)
+            row_total = jnp.sum(near_weights, axis=1, keepdims=True) + jnp.sum(
+                far_weights, axis=1, keepdims=True
+            )
+            weight_ref[block, row_slice, :] = far_weights.astype(jnp.bfloat16)
             total_ref[block, row_slice, :] = jnp.dot(
-                rounded[:, :near_width], v_ref[0, : near_width // BLOCK].reshape(near_width, width), preferred_element_type=jnp.float32
+                near_weights.astype(jnp.bfloat16),
+                v_ref[0, : near_width // BLOCK].reshape(near_width, width),
+                preferred_element_type=jnp.float32,
             )
-            inverse_ref[block, row_slice, :] = jnp.broadcast_to(1.0 / row_total, (rows, width))
+            inverse_ref[block, row_slice, :] = jnp.broadcast_to(1.0 / row_total, (step_rows, width))
             return carry
 
-        lax.fori_loop(0, 8, body, 0)
-
-    score_group(0)
+        lax.fori_loop(0, 2 * steps_per_block, body, 0, unroll=UNROLL)
+
+    score_near(0)
+    score_near(1)
+    second(0)
+    score_near(2)
+    score_near(3)
+    third(0)
+    fourth(0)
+    first(1)
+    last(0)
+
+    score_far(0)
     second(1)
-    score_group(1)
-    score_group(2)
+    score_far(1)
+    score_far(2)
     third(1)
     fourth(1)
-    score_group(3)
+    score_far(3)
     last(1)
 
     x = head // 2
@@ -303,6 +345,7 @@
             pltpu.VMEM((blocks, heads * BLOCK, LEVELS * BLOCK), jnp.bfloat16),
             pltpu.VMEM((blocks, heads, BLOCK, width), jnp.bfloat16),
             pltpu.VMEM((2, 2, heads // 2, BLOCK, width), jnp.bfloat16),
+            *[pltpu.VMEM((2, heads * BLOCK, 2 * BLOCK * (group + 1)), jnp.float32) for group in range(4)],
             pltpu.SemaphoreType.DMA((2, 9)),
             pltpu.SemaphoreType.DMA((2, 9)),
             pltpu.SemaphoreType.DMA((13,)),

time: 84.5 us -> 80 us (0.947)
  Pallas kernels: 81.1 us -> 76.6 us
    pallas_call x1, Pallas kernels: 81.1 us -> 76.6 us  [shards(): pl.pallas_call(kernel, out_shape=jax.ShapeDtypeStruct((heads * head_devic...]
where the time goes in v3:
time: 80 us; the launch traced here: 79.8 us
  Pallas kernels  76.6 us (96%)
  local copies, waits for them, and re-layouts  3.16 us (4%)
    pallas_call x1, Pallas kernels, shards(): pl.pallas_call(kernel, out_shape=jax.ShapeDtypeStruct((heads * head_devic...  76.6 us
    unnamed x1, local copies, waits for them, and re-layouts  3.16 us

profile of v3, /device:TPU:193, one launch (start us, length us, event | category | flops | bytes accessed | tf_op | source)
XLA Modules:
  0.0 79.8 jit_solution(6569590798541963554)
XLA Ops:
  0.0 76.6 %power_attention.1 = bf16[64,128,128]{2,1,0:T(8,128)(2,1)} custom-call(bf16[8,1024,128]{2,1,0:T(8,128)(2,1)} %q_hbm.1, bf16[1,8,128,128]{3,2,1,0:T(8,128)(2,1)} %bitcast.2, bf16[1,8,128,128]{3,2,1,0:T(8,128)(2,1)} %bitcast.3, s32[1,5]{1,0:T(1,128)} %use_ref.1, s32[8,5]{1,0:T(8,128)} %pick_ref.1), custom_call_target="tpu_custom_call" | custom-call | tf_op jit(solution)/shard_map/power_attention/pallas_call | solution.py:332
  76.7 3.2 %copy.7 = bf16[64,128,128]{2,1,0:T(8,128)(2,1)} copy(bf16[64,128,128]{2,1,0:T(8,128)(2,1)} %power_attention.1) | data formatting | bytes 4194304

commit v4 on v3

--- a/solution.py
+++ b/solution.py
@@ -15,7 +15,7 @@
 Y1, Y2, Z1, Z2, Z4F, RELAY, Z4B, Y_RELAY, Y2_BACK = range(9)
 X_COUNT = 4
 STEP_HEADS = 2
-UNROLL = 1
+UNROLL = 2
 DIRECT, SIBLING, LEG1, LEG2 = 0, 4, 5, 9
 
 

time: 80 us -> 77.2 us (0.965)
  Pallas kernels: 76.6 us -> 73.4 us
    pallas_call x1, Pallas kernels: 76.6 us -> 73.4 us  [shards(): pl.pallas_call(kernel, out_shape=jax.ShapeDtypeStruct((heads * head_devic...]
where the time goes in v4:
time: 77.2 us; the launch traced here: 76.5 us
  Pallas kernels  73.4 us (95%)
  local copies, waits for them, and re-layouts  3.16 us (4%)
    pallas_call x1, Pallas kernels, shards(): pl.pallas_call(kernel, out_shape=jax.ShapeDtypeStruct((heads * head_devic...  73.4 us
    unnamed x1, local copies, waits for them, and re-layouts  3.16 us

profile of v4, /device:TPU:193, one launch (start us, length us, event | category | flops | bytes accessed | tf_op | source)
XLA Modules:
  0.0 76.5 jit_solution(18144386405773633157)
XLA Ops:
  0.0 73.4 %power_attention.1 = bf16[64,128,128]{2,1,0:T(8,128)(2,1)} custom-call(bf16[8,1024,128]{2,1,0:T(8,128)(2,1)} %q_hbm.1, bf16[1,8,128,128]{3,2,1,0:T(8,128)(2,1)} %bitcast.2, bf16[1,8,128,128]{3,2,1,0:T(8,128)(2,1)} %bitcast.3, s32[1,5]{1,0:T(1,128)} %use_ref.1, s32[8,5]{1,0:T(8,128)} %pick_ref.1), custom_call_target="tpu_custom_call" | custom-call | tf_op jit(solution)/shard_map/power_attention/pallas_call | solution.py:332
  73.4 3.2 %copy.7 = bf16[64,128,128]{2,1,0:T(8,128)(2,1)} copy(bf16[64,128,128]{2,1,0:T(8,128)(2,1)} %power_attention.1) | data formatting | bytes 4194304

commit v5 on v4

--- a/solution.py
+++ b/solution.py
@@ -237,8 +237,8 @@
     last(0)
 
     score_far(0)
+    score_far(1)
     second(1)
-    score_far(1)
     score_far(2)
     third(1)
     fourth(1)

time: 77.2 us -> 79.6 us (1.031)
  the two profiles are of different devices: /device:TPU:193 before, /device:TPU:225 now
where the time goes in v5:
time: 79.6 us; the launch traced here: 79.5 us
  Pallas kernels  76.3 us (96%)
  local copies, waits for them, and re-layouts  3.16 us (4%)
    pallas_call x1, Pallas kernels, shards(): pl.pallas_call(kernel, out_shape=jax.ShapeDtypeStruct((heads * head_devic...  76.3 us
    unnamed x1, local copies, waits for them, and re-layouts  3.16 us

profile of v5, /device:TPU:225, one launch (start us, length us, event | category | flops | bytes accessed | tf_op | source)
XLA Modules:
  0.0 79.5 jit_solution(12161281412679612507)
XLA Ops:
  0.0 76.3 %power_attention.1 = bf16[64,128,128]{2,1,0:T(8,128)(2,1)} custom-call(bf16[8,1024,128]{2,1,0:T(8,128)(2,1)} %q_hbm.1, bf16[1,8,128,128]{3,2,1,0:T(8,128)(2,1)} %bitcast.2, bf16[1,8,128,128]{3,2,1,0:T(8,128)(2,1)} %bitcast.3, s32[1,5]{1,0:T(1,128)} %use_ref.1, s32[8,5]{1,0:T(8,128)} %pick_ref.1), custom_call_target="tpu_custom_call" | custom-call | tf_op jit(solution)/shard_map/power_attention/pallas_call | solution.py:332
  76.3 3.2 %copy.7 = bf16[64,128,128]{2,1,0:T(8,128)(2,1)} copy(bf16[64,128,128]{2,1,0:T(8,128)(2,1)} %power_attention.1) | data formatting | bytes 4194304
